TPU v7x, 32 devices: a whole 2x2x4 slice. The times are simulated.
32 devices in a mesh: rows: 32 (over z, y, x, core).
Axes of the slice: x: 2, y: 2, z: 4, core: 2. Of those that a mesh axis runs over, the one named last changes fastest.
Arguments:
- points: float32 [8, 131072], P(None, 'rows'), may hold values from -6 to 6
- scales: float32 [8], replicated, may hold values from 1 to 3
- noise_var: float32 [131072], P('rows'), may hold values from 0.05 to 0.5
- pivots: int32 [8, 16], replicated, may hold values from 0 to 131071, as said below
Outputs:
- factor: float32 [128, 131072], P(None, 'rows')
- residual_diag: float32 [131072], P('rows')
- mean_residual: float32 [8], replicated
Inputs may be any that keep to these rules, and one draw needn't show every extreme that they name: `pivots`: all 128 entries are distinct point indices.
All inputs are finite; a program needn't handle non-finite values.
Results may differ from a plain program's by a relative error of at most 0.00014.
Values sent between devices are 32-bit elements; how exact they have to be, the bound alone decides.
A program may use at most 64 MiB of HBM per device.

v0:
```python
import functools

import jax
import jax.numpy as jnp
from jax import lax
from jax.experimental import pallas as pl
from jax.experimental.pallas import tpu as pltpu
from jax.sharding import PartitionSpec as P

LANES = 128
SUB = 8
F32 = jnp.float32
BF16 = jnp.bfloat16


def split3(x):
    high = x.astype(BF16).astype(F32)
    rest = x - high
    mid = rest.astype(BF16).astype(F32)
    low = (rest - mid).astype(BF16).astype(F32)
    return high, mid, low


def load_points(dim, points, scales, noise, packed):
    axis_pos = lax.broadcasted_iota(jnp.int32, (dim, 1), 0)
    scale = jnp.ones((dim, 1), F32)
    for d in range(dim):
        scale = jnp.where(axis_pos == d, scales[d], scale)
    packed[0:dim, :] = points[...] / scale
    packed[dim : 2 * dim, :] = jnp.broadcast_to(noise[...], (dim, noise.shape[1]))


def gather_own(ranks, offset, chunk, pivot_row, packed):
    rows, width = packed.shape
    wanted = pivot_row - offset
    acc = jnp.zeros((3 * rows, ranks), F32)
    for c in range(width // chunk):
        pieces = jnp.concatenate(split3(packed[:, c * chunk : (c + 1) * chunk]), axis=0)
        ids = lax.broadcasted_iota(jnp.int32, (chunk, ranks), 0) + c * chunk
        hot = jnp.where(ids == wanted, 1.0, 0.0).astype(BF16)
        acc = acc + jnp.dot(pieces.astype(BF16), hot, preferred_element_type=F32)
    return acc[0:rows] + acc[rows : 2 * rows] + acc[2 * rows :]


def exchange_start(n, me, slots, send_sem, recv_sem):
    def send(k, carry):
        pltpu.make_async_remote_copy(
            src_ref=slots.at[0],
            dst_ref=slots.at[k],
            send_sem=send_sem.at[k],
            recv_sem=recv_sem.at[k],
            device_id=(lax.rem(me + k, n),),
            device_id_type=pl.DeviceIdType.MESH,
        ).start()
        return carry

    lax.fori_loop(1, n, send, 0)


def exchange_finish(n, me, slots, send_sem, recv_sem):
    def collect(k, total):
        pltpu.make_async_remote_copy(
            src_ref=slots.at[0],
            dst_ref=slots.at[k],
            send_sem=send_sem.at[k],
            recv_sem=recv_sem.at[k],
            device_id=(lax.rem(me + k, n),),
            device_id_type=pl.DeviceIdType.MESH,
        ).wait()
        return total + slots[k]

    return lax.fori_loop(1, n, collect, slots[0])


def pivot_covariance(dim, coords):
    ranks = coords.shape[1]
    across = coords.T
    total = jnp.zeros((ranks, ranks), F32)
    for d in range(dim):
        differ = across[:, d : d + 1] - coords[d : d + 1, :]
        total = total + differ * differ
    row = lax.broadcasted_iota(jnp.int32, (ranks, ranks), 0)
    col = lax.broadcasted_iota(jnp.int32, (ranks, ranks), 1)
    cov = jnp.exp(-0.5 * total) + jnp.where(row == col, coords[dim : dim + 1, :], 0.0)
    return cov, (row == col).astype(F32)


def eliminate(left, right, first_lane):
    shape = left[0].shape
    a = [
        [
            jnp.broadcast_to(left[i][:, first_lane + j : first_lane + j + 1], shape)
            for j in range(i + 1)
        ]
        for i in range(SUB)
    ]
    inverse = []
    for k in range(SUB):
        r = lax.rsqrt(a[k][k])
        inverse.append(r)
        left[k] = left[k] * r
        right[k] = right[k] * r
        for i in range(k + 1, SUB):
            a[i][k] = a[i][k] * r
        for i in range(k + 1, SUB):
            for j in range(k + 1, i + 1):
                a[i][j] = a[i][j] - a[i][k] * a[j][k]
            left[i] = left[i] - a[i][k] * left[k]
            right[i] = right[i] - a[i][k] * right[k]
    return a, inverse


def spread(rows):
    return [jnp.broadcast_to(rows[i : i + 1], rows.shape) for i in range(SUB)]


def gathered(rows):
    return jnp.concatenate([rows[i][i : i + 1] for i in range(SUB)], axis=0)


def factor_rows(ranks, state):
    step = 2 * SUB
    for lo in range(0, ranks, step):
        mid, hi = lo + SUB, lo + step
        left = spread(state[lo:mid, 0:ranks])
        right = spread(state[lo:mid, ranks : 2 * ranks])
        low_left = state[mid:hi, 0:ranks]
        low_right = state[mid:hi, ranks : 2 * ranks]
        start = [
            jnp.broadcast_to(low_left[:, lo + k : lo + k + 1], (SUB, ranks))
            for k in range(SUB)
        ]
        mult, inverse = eliminate(left, right, lo)
        cols = []
        for k in range(SUB):
            col = start[k]
            for j in range(k):
                col = col - cols[j] * mult[k][j]
            cols.append(col * inverse[k])
        for k in range(SUB):
            low_left = low_left - cols[k] * left[k]
            low_right = low_right - cols[k] * right[k]
        next_left, next_right = spread(low_left), spread(low_right)
        eliminate(next_left, next_right, mid)
        new_left = jnp.concatenate([gathered(left), gathered(next_left)], axis=0)
        new_right = jnp.concatenate([gathered(right), gathered(next_right)], axis=0)
        state[lo:hi, ranks : 2 * ranks] = new_right
        if hi < ranks:
            new = jnp.concatenate([new_left, new_right], axis=1)
            h, m, l = split3(new)
            lh, lm, ll = (x[:, 0:ranks] for x in (h, m, l))
            one = jnp.concatenate([lh, lh, lh, lm, lm, ll], axis=0).T[hi:ranks].astype(BF16)
            two = jnp.concatenate([h, m, l, h, m, h], axis=0).astype(BF16)
            state[hi:ranks, :] = state[hi:ranks, :] - jnp.dot(
                one, two, preferred_element_type=F32
            )


def pivot_side(dim, coords, centre):
    y = coords[0:dim, :] - centre
    yh, ym, yl = split3(y)
    nh, nm, nl = split3(-0.5 * jnp.sum(y * y, axis=0, keepdims=True))
    ones = jnp.ones_like(nh)
    tail = [ones, ones, ones, nh, nm, nl, jnp.zeros((dim - 6, y.shape[1]), F32)]
    return jnp.concatenate([yh, yh, ym, ym, yh, yl] + tail, axis=0).T.astype(BF16)


def point_side(dim, x):
    xh, xm, xl = split3(x)
    nh, nm, nl = split3(-0.5 * jnp.sum(x * x, axis=0, keepdims=True))
    ones = jnp.ones_like(nh)
    tail = [nh, nm, nl, ones, ones, ones, jnp.zeros((dim - 6, x.shape[1]), F32)]
    return jnp.concatenate([xh, xm, xh, xm, xl, xh] + tail, axis=0).astype(BF16)


def body_kernel(
    n, blocks, chunk,
    points, scales, noise, pivots,
    factor, residual, averages,
    packed, slots, state, after, sum_slots,
    send_sem, recv_sem, sum_send_sem, sum_recv_sem,
):
    dim, width = points.shape
    ranks = factor.shape[0]
    per_block = ranks // blocks
    me = lax.axis_index("rows")
    offset = me * width

    barrier = pltpu.get_barrier_semaphore()

    def greet(k, carry):
        pl.semaphore_signal(
            barrier, inc=1, device_id=(lax.rem(me + k, n),),
            device_id_type=pl.DeviceIdType.MESH,
        )
        return carry

    lax.fori_loop(1, n, greet, 0)
    load_points(dim, points, scales, noise, packed)
    pivot_row = jnp.concatenate([pivots[b : b + 1, :] for b in range(blocks)], axis=1)
    own = gather_own(ranks, offset, chunk, pivot_row, packed)
    for d in range(dim + 1):
        slots[0, d] = own[d : d + 1]
    pl.semaphore_wait(barrier, n - 1)
    exchange_start(n, me, slots, send_sem, recv_sem)
    coords = exchange_finish(n, me, slots, send_sem, recv_sem)
    coords = jnp.concatenate([coords[d] for d in range(dim + 1)], axis=0)

    cov, eye = pivot_covariance(dim, coords)
    state[:, 0:ranks] = cov
    state[:, ranks : 2 * ranks] = eye
    factor_rows(ranks, state)
    row = lax.broadcasted_iota(jnp.int32, (ranks, ranks), 0)
    col = lax.broadcasted_iota(jnp.int32, (ranks, ranks), 1)
    solve = jnp.where(row >= col, state[:, ranks : 2 * ranks], 0.0)

    centre = jnp.sum(coords[0:dim, :], axis=1, keepdims=True) / ranks
    side = pivot_side(dim, coords, centre)
    local_row = (pivot_row - offset).astype(F32)
    local_col = jnp.broadcast_to(local_row, (SUB, ranks)).T[:, 0:1].astype(jnp.int32)
    for c in range(width // chunk):
        at = slice(c * chunk, (c + 1) * chunk)
        x = packed[0:dim, at] - centre
        cross = jnp.exp(jnp.dot(side, point_side(dim, x), preferred_element_type=F32))
        noise_row = packed[dim : dim + 1, at]
        ids = lax.broadcasted_iota(jnp.int32, (ranks, chunk), 1) + c * chunk
        cross = cross + jnp.where(ids == local_col, noise_row, 0.0)
        rows = jnp.dot(
            solve, cross, precision=lax.Precision.HIGHEST, preferred_element_type=F32
        )
        factor[:, at] = rows
        left = 1.0 + noise_row
        for b in range(blocks):
            part = rows[b * per_block : (b + 1) * per_block]
            left = left - jnp.sum(part * part, axis=0, keepdims=True)
            after[b : b + 1, at] = left
        residual[at] = left[0]

    total = jnp.zeros((blocks, LANES), F32)
    for c in range(width // LANES):
        total = total + after[:, c * LANES : (c + 1) * LANES]
    total = jnp.sum(total, axis=1, keepdims=True)
    row = lax.broadcasted_iota(jnp.int32, (blocks, LANES), 0)
    col = lax.broadcasted_iota(jnp.int32, (blocks, LANES), 1)
    sum_slots[0] = jnp.sum(jnp.where(row == col, total, 0.0), axis=0, keepdims=True)
    exchange_start(n, me, sum_slots, sum_send_sem, sum_recv_sem)
    total = exchange_finish(n, me, sum_slots, sum_send_sem, sum_recv_sem)
    averages[...] = total[0, 0:blocks] / (width * n)


def store_kernel(factor, residual, averages, to_factor, to_residual, to_averages, sem):
    copies = [
        pltpu.make_async_copy(source, target, sem.at[i])
        for i, (source, target) in enumerate(
            [(factor, to_factor), (residual, to_residual), (averages, to_averages)]
        )
    ]
    for copy in copies:
        copy.start()
    for copy in copies:
        copy.wait()


def body(n, points, scales, noise_var, pivots):
    dim, width = points.shape
    blocks, per_block = pivots.shape
    ranks = blocks * per_block
    chunk = 512
    vmem = pl.BlockSpec(memory_space=pltpu.VMEM)
    factor, residual, averages = pl.pallas_call(
        functools.partial(body_kernel, n, blocks, chunk),
        name="whole",
        out_shape=(
            pltpu.VMEM((ranks, width), F32),
            pltpu.VMEM((width,), F32),
            pltpu.VMEM((blocks,), F32),
        ),
        in_specs=[
            vmem, pl.BlockSpec(memory_space=pltpu.SMEM), vmem, vmem,
        ],
        out_specs=(vmem, vmem, vmem),
        scratch_shapes=[
            pltpu.VMEM((2 * dim, width), F32),
            pltpu.VMEM((n, dim + 1, 1, ranks), F32),
            pltpu.VMEM((ranks, 2 * ranks), F32),
            pltpu.VMEM((blocks, width), F32),
            pltpu.VMEM((n, 1, LANES), F32),
            pltpu.SemaphoreType.DMA((n,)),
            pltpu.SemaphoreType.DMA((n,)),
            pltpu.SemaphoreType.DMA((n,)),
            pltpu.SemaphoreType.DMA((n,)),
        ],
        compiler_params=pltpu.CompilerParams(collective_id=0, has_side_effects=True),
    )(points, scales, noise_var.reshape(1, -1), pivots)
    anywhere = pl.BlockSpec(memory_space=pl.ANY)
    return pl.pallas_call(
        store_kernel,
        name="store",
        out_shape=(
            jax.ShapeDtypeStruct((ranks, width), F32),
            jax.ShapeDtypeStruct((width,), F32),
            jax.ShapeDtypeStruct((blocks,), F32),
        ),
        in_specs=[vmem] * 3,
        out_specs=(anywhere,) * 3,
        scratch_shapes=[pltpu.SemaphoreType.DMA((3,))],
    )(*(pltpu.with_memory_space_constraint(x, pltpu.VMEM) for x in (factor, residual, averages)))


def solution(mesh):
    in_specs = (P(None, "rows"), P(), P("rows"), P())
    out_specs = (P(None, "rows"), P("rows"), P())
    return jax.shard_map(
        functools.partial(body, mesh.shape["rows"]),
        mesh=mesh, in_specs=in_specs, out_specs=out_specs, check_vma=False,
    )
```

profile of v0, /device:TPU:0, one launch (start us, length us, event | category | flops | bytes accessed | tf_op | source)
XLA Modules:
  0.0 29.9 jit_solution(16096990109169777456)
XLA Ops:
  0.6 28.0 %whole.1 = (f32[128,4096]{1,0:T(8,128)S(1)}, f32[4096]{0:T(1024)S(1)}, f32[8]{0:T(128)S(1)}) custom-call(f32[8,4096]{1,0:T(8,128)} %points.1, f32[8]{0:T(128)} %scales.1, f32[1,4096]{1,0:T(1,128)} %bitcast.1, s32[8,16]{1,0:T(8,128)} %pivots.1), custom_call_target="tpu_custom_call" | custom-call | tf_op jit(solution)/shard_map/whole/pallas_call | solution.py:270
  28.6 1.4 %store.1 = (f32[128,4096]{1,0:T(8,128)}, f32[4096]{0:T(1024)}, f32[8]{0:T(128)}) custom-call(f32[128,4096]{1,0:T(8,128)S(1)} %get-tuple-element.6.factor, f32[4096]{0:T(1024)S(1)} %get-tuple-element.7.residual, f32[8]{0:T(128)S(1)} %get-tuple-element.8.averages), custom_call_target="tpu_custom_call" | custom-call | tf_op jit(solution)/shard_map/store/pallas_call | solution.py:296
where the time goes:
time: 30.1 us; the launch traced here: 29.9 us
  Pallas kernels  29.3 us (97%)
  between operations  0.64 us (2%)
    pallas_call x1, Pallas kernels, body(): pl.pallas_call(functools.partial(body_kernel, n, blocks, chunk), name='wh...  28 us
    pallas_call x1, Pallas kernels, body(): pl.pallas_call(store_kernel, name='store', out_shape=(jax.ShapeDtypeStruc...  1.35 us

commit v1 on v0

--- a/solution.py
+++ b/solution.py
@@ -21,55 +21,75 @@
     return high, mid, low
 
 
-def load_points(dim, points, scales, noise, packed):
+def load_points(dim, points, scale, noise, packed):
+    packed[0:dim, :] = points[...] / scale
+    packed[dim : 2 * dim, :] = jnp.broadcast_to(noise[...], (dim, noise.shape[1]))
+
+
+def scale_column(dim, scales):
     axis_pos = lax.broadcasted_iota(jnp.int32, (dim, 1), 0)
     scale = jnp.ones((dim, 1), F32)
     for d in range(dim):
         scale = jnp.where(axis_pos == d, scales[d], scale)
-    packed[0:dim, :] = points[...] / scale
-    packed[dim : 2 * dim, :] = jnp.broadcast_to(noise[...], (dim, noise.shape[1]))
-
-
-def gather_own(ranks, offset, chunk, pivot_row, packed):
-    rows, width = packed.shape
-    wanted = pivot_row - offset
-    acc = jnp.zeros((3 * rows, ranks), F32)
-    for c in range(width // chunk):
-        pieces = jnp.concatenate(split3(packed[:, c * chunk : (c + 1) * chunk]), axis=0)
-        ids = lax.broadcasted_iota(jnp.int32, (chunk, ranks), 0) + c * chunk
-        hot = jnp.where(ids == wanted, 1.0, 0.0).astype(BF16)
-        acc = acc + jnp.dot(pieces.astype(BF16), hot, preferred_element_type=F32)
-    return acc[0:rows] + acc[rows : 2 * rows] + acc[2 * rows :]
-
-
-def exchange_start(n, me, slots, send_sem, recv_sem):
-    def send(k, carry):
+    return scale
+
+
+def gather_own(offset, pivot_row, points, noise_tiles):
+    dim, width = points.shape
+    ranks = pivot_row.shape[1]
+    wanted = jnp.broadcast_to(pivot_row - offset, (SUB, ranks))
+    lane = jnp.bitwise_and(wanted, LANES - 1)
+    tile = jnp.right_shift(wanted, 7)
+    own = jnp.zeros((dim, ranks), F32)
+    for t in range(width // LANES):
+        part = points[:, t * LANES : (t + 1) * LANES]
+        own = jnp.where(tile == t, jnp.take_along_axis(part, lane, axis=1), own)
+    row = lax.broadcasted_iota(jnp.int32, (SUB, ranks), 0)
+    own_noise = jnp.zeros((SUB, ranks), F32)
+    for t in range(0, width // LANES, SUB):
+        part = noise_tiles[t : t + SUB, :]
+        own_noise = jnp.where(
+            tile == row + t, jnp.take_along_axis(part, lane, axis=1), own_noise
+        )
+    return own, jnp.sum(own_noise, axis=0, keepdims=True)
+
+
+def partners(n, group, me):
+    low, high = lax.rem(me, group), me - lax.rem(me, group)
+    near = [high + lax.rem(low + k, group) for k in range(1, group)]
+    far = [lax.rem(me + k * group, n) for k in range(1, n // group)]
+    return near, far
+
+
+def exchange(devices, slots, send_sem, recv_sem):
+    for k, device in enumerate(devices):
         pltpu.make_async_remote_copy(
             src_ref=slots.at[0],
-            dst_ref=slots.at[k],
-            send_sem=send_sem.at[k],
-            recv_sem=recv_sem.at[k],
-            device_id=(lax.rem(me + k, n),),
+            dst_ref=slots.at[k + 1],
+            send_sem=send_sem,
+            recv_sem=recv_sem,
+            device_id=(device,),
             device_id_type=pl.DeviceIdType.MESH,
         ).start()
-        return carry
-
-    lax.fori_loop(1, n, send, 0)
-
-
-def exchange_finish(n, me, slots, send_sem, recv_sem):
-    def collect(k, total):
-        pltpu.make_async_remote_copy(
-            src_ref=slots.at[0],
-            dst_ref=slots.at[k],
-            send_sem=send_sem.at[k],
-            recv_sem=recv_sem.at[k],
-            device_id=(lax.rem(me + k, n),),
-            device_id_type=pl.DeviceIdType.MESH,
-        ).wait()
-        return total + slots[k]
-
-    return lax.fori_loop(1, n, collect, slots[0])
+
+
+def all_of(devices, slots, send_sem, recv_sem):
+    rest = slots.at[pl.ds(1, len(devices))]
+    return pltpu.make_async_remote_copy(
+        src_ref=rest,
+        dst_ref=rest,
+        send_sem=send_sem,
+        recv_sem=recv_sem,
+        device_id=(devices[0],),
+        device_id_type=pl.DeviceIdType.MESH,
+    )
+
+
+def total_of(slots):
+    total = slots[0]
+    for k in range(1, slots.shape[0]):
+        total = total + slots[k]
+    return total
 
 
 def pivot_covariance(dim, coords):
@@ -174,36 +194,41 @@
 
 
 def body_kernel(
-    n, blocks, chunk,
-    points, scales, noise, pivots,
+    n, group, blocks, chunk,
+    points, scales, noise, noise_tiles, pivots,
     factor, residual, averages,
-    packed, slots, state, after, sum_slots,
-    send_sem, recv_sem, sum_send_sem, sum_recv_sem,
+    packed, near_slots, far_slots, state, after, near_sums, far_sums,
+    send_sem, recv_sem,
 ):
     dim, width = points.shape
     ranks = factor.shape[0]
     per_block = ranks // blocks
     me = lax.axis_index("rows")
     offset = me * width
+    near, far = partners(n, group, me)
 
     barrier = pltpu.get_barrier_semaphore()
-
-    def greet(k, carry):
+    for device in near + far:
         pl.semaphore_signal(
-            barrier, inc=1, device_id=(lax.rem(me + k, n),),
-            device_id_type=pl.DeviceIdType.MESH,
+            barrier, inc=1, device_id=(device,), device_id_type=pl.DeviceIdType.MESH
         )
-        return carry
-
-    lax.fori_loop(1, n, greet, 0)
-    load_points(dim, points, scales, noise, packed)
+    scale = scale_column(dim, scales)
     pivot_row = jnp.concatenate([pivots[b : b + 1, :] for b in range(blocks)], axis=1)
-    own = gather_own(ranks, offset, chunk, pivot_row, packed)
-    for d in range(dim + 1):
-        slots[0, d] = own[d : d + 1]
-    pl.semaphore_wait(barrier, n - 1)
-    exchange_start(n, me, slots, send_sem, recv_sem)
-    coords = exchange_finish(n, me, slots, send_sem, recv_sem)
+    own, own_noise = gather_own(offset, pivot_row, points, noise_tiles)
+    own = own / scale
+    for d in range(dim):
+        near_slots[0, d] = own[d : d + 1]
+    near_slots[0, dim] = own_noise
+    pl.semaphore_wait(barrier, len(near) + len(far))
+    first = (near, near_slots, send_sem.at[0], recv_sem.at[0])
+    second = (far, far_slots, send_sem.at[1], recv_sem.at[1])
+    exchange(*first)
+    load_points(dim, points, scale, noise, packed)
+    all_of(*first).wait_recv()
+    far_slots[0] = total_of(near_slots)
+    exchange(*second)
+    all_of(*second).wait_recv()
+    coords = total_of(far_slots)
     coords = jnp.concatenate([coords[d] for d in range(dim + 1)], axis=0)
 
     cov, eye = pivot_covariance(dim, coords)
@@ -242,9 +267,17 @@
     total = jnp.sum(total, axis=1, keepdims=True)
     row = lax.broadcasted_iota(jnp.int32, (blocks, LANES), 0)
     col = lax.broadcasted_iota(jnp.int32, (blocks, LANES), 1)
-    sum_slots[0] = jnp.sum(jnp.where(row == col, total, 0.0), axis=0, keepdims=True)
-    exchange_start(n, me, sum_slots, sum_send_sem, sum_recv_sem)
-    total = exchange_finish(n, me, sum_slots, sum_send_sem, sum_recv_sem)
+    near_sums[0] = jnp.sum(jnp.where(row == col, total, 0.0), axis=0, keepdims=True)
+    third = (near, near_sums, send_sem.at[2], recv_sem.at[2])
+    fourth = (far, far_sums, send_sem.at[3], recv_sem.at[3])
+    exchange(*third)
+    all_of(*third).wait_recv()
+    far_sums[0] = total_of(near_sums)
+    exchange(*fourth)
+    all_of(*fourth).wait_recv()
+    total = total_of(far_sums)
+    for step in (first, second, third, fourth):
+        all_of(*step).wait_send()
     averages[...] = total[0, 0:blocks] / (width * n)
 
 
@@ -266,9 +299,12 @@
     blocks, per_block = pivots.shape
     ranks = blocks * per_block
     chunk = 512
+    group = 1
+    while group * group < n:
+        group *= 2
     vmem = pl.BlockSpec(memory_space=pltpu.VMEM)
     factor, residual, averages = pl.pallas_call(
-        functools.partial(body_kernel, n, blocks, chunk),
+        functools.partial(body_kernel, n, group, blocks, chunk),
         name="whole",
         out_shape=(
             pltpu.VMEM((ranks, width), F32),
@@ -276,22 +312,22 @@
             pltpu.VMEM((blocks,), F32),
         ),
         in_specs=[
-            vmem, pl.BlockSpec(memory_space=pltpu.SMEM), vmem, vmem,
+            vmem, pl.BlockSpec(memory_space=pltpu.SMEM), vmem, vmem, vmem,
         ],
         out_specs=(vmem, vmem, vmem),
         scratch_shapes=[
             pltpu.VMEM((2 * dim, width), F32),
-            pltpu.VMEM((n, dim + 1, 1, ranks), F32),
+            pltpu.VMEM((group, dim + 1, 1, ranks), F32),
+            pltpu.VMEM((n // group, dim + 1, 1, ranks), F32),
             pltpu.VMEM((ranks, 2 * ranks), F32),
             pltpu.VMEM((blocks, width), F32),
-            pltpu.VMEM((n, 1, LANES), F32),
-            pltpu.SemaphoreType.DMA((n,)),
-            pltpu.SemaphoreType.DMA((n,)),
-            pltpu.SemaphoreType.DMA((n,)),
-            pltpu.SemaphoreType.DMA((n,)),
+            pltpu.VMEM((group, 1, LANES), F32),
+            pltpu.VMEM((n // group, 1, LANES), F32),
+            pltpu.SemaphoreType.DMA((4,)),
+            pltpu.SemaphoreType.DMA((4,)),
         ],
         compiler_params=pltpu.CompilerParams(collective_id=0, has_side_effects=True),
-    )(points, scales, noise_var.reshape(1, -1), pivots)
+    )(points, scales, noise_var.reshape(1, -1), noise_var.reshape(-1, LANES), pivots)
     anywhere = pl.BlockSpec(memory_space=pl.ANY)
     return pl.pallas_call(
         store_kernel,

time: 30.1 us -> 29.8 us (0.990)
  no operation moved by 1% of the time
where the time goes in v1:
time: 29.8 us; the launch traced here: 29.7 us
  Pallas kernels  29 us (97%)
  between operations  0.64 us (2%)
    pallas_call x1, Pallas kernels, body(): pl.pallas_call(functools.partial(body_kernel, n, group, blocks, chunk), n...  27.7 us
    pallas_call x1, Pallas kernels, body(): pl.pallas_call(store_kernel, name='store', out_shape=(jax.ShapeDtypeStruc...  1.35 us

profile of v1, /device:TPU:0, one launch (start us, length us, event | category | flops | bytes accessed | tf_op | source)
XLA Modules:
  0.0 29.7 jit_solution(5928153521012610967)
XLA Ops:
  0.6 27.7 %whole.1 = (f32[128,4096]{1,0:T(8,128)S(1)}, f32[4096]{0:T(1024)S(1)}, f32[8]{0:T(128)S(1)}) custom-call(f32[8,4096]{1,0:T(8,128)} %points.1, f32[8]{0:T(128)} %scales.1, f32[1,4096]{1,0:T(1,128)} %bitcast.2, f32[32,128]{1,0:T(8,128)} %bitcast.3, s32[8,16]{1,0:T(8,128)} %pivots.1), custom_call_target="tpu_custom_call" | custom-call | tf_op jit(solution)/shard_map/whole/pallas_call | solution.py:306
  28.3 1.4 %store.1 = (f32[128,4096]{1,0:T(8,128)}, f32[4096]{0:T(1024)}, f32[8]{0:T(128)}) custom-call(f32[128,4096]{1,0:T(8,128)S(1)} %get-tuple-element.6.factor, f32[4096]{0:T(1024)S(1)} %get-tuple-element.7.residual, f32[8]{0:T(128)S(1)} %get-tuple-element.8.averages), custom_call_target="tpu_custom_call" | custom-call | tf_op jit(solution)/shard_map/store/pallas_call | solution.py:332

commit v2 on v1

--- a/solution.py
+++ b/solution.py
@@ -19,11 +19,6 @@
     mid = rest.astype(BF16).astype(F32)
     low = (rest - mid).astype(BF16).astype(F32)
     return high, mid, low
-
-
-def load_points(dim, points, scale, noise, packed):
-    packed[0:dim, :] = points[...] / scale
-    packed[dim : 2 * dim, :] = jnp.broadcast_to(noise[...], (dim, noise.shape[1]))
 
 
 def scale_column(dim, scales):
@@ -52,44 +47,6 @@
             tile == row + t, jnp.take_along_axis(part, lane, axis=1), own_noise
         )
     return own, jnp.sum(own_noise, axis=0, keepdims=True)
-
-
-def partners(n, group, me):
-    low, high = lax.rem(me, group), me - lax.rem(me, group)
-    near = [high + lax.rem(low + k, group) for k in range(1, group)]
-    far = [lax.rem(me + k * group, n) for k in range(1, n // group)]
-    return near, far
-
-
-def exchange(devices, slots, send_sem, recv_sem):
-    for k, device in enumerate(devices):
-        pltpu.make_async_remote_copy(
-            src_ref=slots.at[0],
-            dst_ref=slots.at[k + 1],
-            send_sem=send_sem,
-            recv_sem=recv_sem,
-            device_id=(device,),
-            device_id_type=pl.DeviceIdType.MESH,
-        ).start()
-
-
-def all_of(devices, slots, send_sem, recv_sem):
-    rest = slots.at[pl.ds(1, len(devices))]
-    return pltpu.make_async_remote_copy(
-        src_ref=rest,
-        dst_ref=rest,
-        send_sem=send_sem,
-        recv_sem=recv_sem,
-        device_id=(devices[0],),
-        device_id_type=pl.DeviceIdType.MESH,
-    )
-
-
-def total_of(slots):
-    total = slots[0]
-    for k in range(1, slots.shape[0]):
-        total = total + slots[k]
-    return total
 
 
 def pivot_covariance(dim, coords):
@@ -138,7 +95,7 @@
     return jnp.concatenate([rows[i][i : i + 1] for i in range(SUB)], axis=0)
 
 
-def factor_rows(ranks, state):
+def factor_rows(ranks, state, between):
     step = 2 * SUB
     for lo in range(0, ranks, step):
         mid, hi = lo + SUB, lo + step
@@ -174,6 +131,7 @@
             state[hi:ranks, :] = state[hi:ranks, :] - jnp.dot(
                 one, two, preferred_element_type=F32
             )
+        between(lo // step)
 
 
 def pivot_side(dim, coords, centre):
@@ -181,7 +139,7 @@
     yh, ym, yl = split3(y)
     nh, nm, nl = split3(-0.5 * jnp.sum(y * y, axis=0, keepdims=True))
     ones = jnp.ones_like(nh)
-    tail = [ones, ones, ones, nh, nm, nl, jnp.zeros((dim - 6, y.shape[1]), F32)]
+    tail = [ones, ones, ones, nh, nm, nl, jnp.zeros((2 * dim - 6, y.shape[1]), F32)]
     return jnp.concatenate([yh, yh, ym, ym, yh, yl] + tail, axis=0).T.astype(BF16)
 
 
@@ -189,29 +147,89 @@
     xh, xm, xl = split3(x)
     nh, nm, nl = split3(-0.5 * jnp.sum(x * x, axis=0, keepdims=True))
     ones = jnp.ones_like(nh)
-    tail = [nh, nm, nl, ones, ones, ones, jnp.zeros((dim - 6, x.shape[1]), F32)]
+    tail = [nh, nm, nl, ones, ones, ones, jnp.zeros((2 * dim - 6, x.shape[1]), F32)]
     return jnp.concatenate([xh, xm, xh, xm, xl, xh] + tail, axis=0).astype(BF16)
+
+
+def send(slots, k, device, send_sem, recv_sem):
+    pltpu.make_async_remote_copy(
+        src_ref=slots.at[0],
+        dst_ref=slots.at[k],
+        send_sem=send_sem,
+        recv_sem=recv_sem,
+        device_id=(device,),
+        device_id_type=pl.DeviceIdType.MESH,
+    ).start()
+
+
+def all_of(slots, device, send_sem, recv_sem):
+    rest = slots.at[pl.ds(1, slots.shape[0] - 1)]
+    return pltpu.make_async_remote_copy(
+        src_ref=rest,
+        dst_ref=rest,
+        send_sem=send_sem,
+        recv_sem=recv_sem,
+        device_id=(device,),
+        device_id_type=pl.DeviceIdType.MESH,
+    )
+
+
+def total_of(slots):
+    parts = [slots[k] for k in range(slots.shape[0])]
+    while len(parts) > 1:
+        parts = [a + b for a, b in zip(parts[::2], parts[1::2])] + (
+            parts[-1:] if len(parts) % 2 else []
+        )
+    return parts[0]
+
+
+def signal(sem, device):
+    pl.semaphore_signal(
+        sem, inc=1, device_id=(device,), device_id_type=pl.DeviceIdType.MESH
+    )
 
 
 def body_kernel(
     n, group, blocks, chunk,
+    from_points, from_scales, from_noise, from_tiles, from_pivots,
+    factor, residual, averages,
     points, scales, noise, noise_tiles, pivots,
-    factor, residual, averages,
-    packed, near_slots, far_slots, state, after, near_sums, far_sums,
-    send_sem, recv_sem,
+    near_slots, far_slots, sum_slots, state, sides, pieces,
+    load_sem, send_sem, recv_sem, ready_sem,
 ):
     dim, width = points.shape
     ranks = factor.shape[0]
     per_block = ranks // blocks
     me = lax.axis_index("rows")
     offset = me * width
-    near, far = partners(n, group, me)
-
+    far_count = n // group
+    low = lax.rem(me, group)
+    level = (me - low) // group
+    near = [me - low + lax.rem(low + k, group) for k in range(1, group)]
+    far = [lax.rem(me + k * group, n) for k in range(1, far_count)]
+
+    loads = [
+        pltpu.make_async_copy(source, target, load_sem.at[i])
+        for i, (source, target) in enumerate(
+            [
+                (from_points, points), (from_scales, scales), (from_noise, noise),
+                (from_tiles, noise_tiles), (from_pivots, pivots),
+            ]
+        )
+    ]
+    for load in loads:
+        load.start()
     barrier = pltpu.get_barrier_semaphore()
-    for device in near + far:
-        pl.semaphore_signal(
-            barrier, inc=1, device_id=(device,), device_id_type=pl.DeviceIdType.MESH
-        )
+    for device in near:
+        signal(barrier, device)
+    for k in range(1, far_count):
+
+        @pl.when(level + k < far_count)
+        def _():
+            signal(barrier, me + k * group)
+
+    for load in loads:
+        load.wait()
     scale = scale_column(dim, scales)
     pivot_row = jnp.concatenate([pivots[b : b + 1, :] for b in range(blocks)], axis=1)
     own, own_noise = gather_own(offset, pivot_row, points, noise_tiles)
@@ -219,66 +237,115 @@
     for d in range(dim):
         near_slots[0, d] = own[d : d + 1]
     near_slots[0, dim] = own_noise
-    pl.semaphore_wait(barrier, len(near) + len(far))
-    first = (near, near_slots, send_sem.at[0], recv_sem.at[0])
-    second = (far, far_slots, send_sem.at[1], recv_sem.at[1])
-    exchange(*first)
-    load_points(dim, points, scale, noise, packed)
-    all_of(*first).wait_recv()
+    pl.semaphore_wait(barrier, group - 1 + level)
+    for k, device in enumerate(near):
+        send(near_slots, k + 1, device, send_sem.at[0], recv_sem.at[0])
+    for k in range(1, far_count):
+
+        @pl.when(level >= k)
+        def _():
+            signal(ready_sem, me - k * group)
+
+    centre = jnp.sum(points[...], axis=1, keepdims=True) / (width * scale)
+    base = jnp.zeros((SUB, LANES), F32)
+    for t in range(0, width // LANES, SUB):
+        base = base + (1.0 + noise_tiles[t : t + SUB, :])
+    base = jnp.sum(jnp.sum(base, axis=1, keepdims=True), axis=0, keepdims=True)
+    for c in range(width // chunk):
+        at = slice(c * chunk, (c + 1) * chunk)
+        sides[:, at] = point_side(dim, points[:, at] / scale - centre)
+
+    all_of(near_slots, near[0], send_sem.at[0], recv_sem.at[0]).wait_recv()
     far_slots[0] = total_of(near_slots)
-    exchange(*second)
-    all_of(*second).wait_recv()
+
+    @pl.when(level < far_count - 1)
+    def _():
+        pl.semaphore_wait(ready_sem, far_count - 1 - level)
+
+    for k, device in enumerate(far):
+        send(far_slots, k + 1, device, send_sem.at[1], recv_sem.at[1])
+    all_of(far_slots, far[0], send_sem.at[1], recv_sem.at[1]).wait_recv()
     coords = total_of(far_slots)
     coords = jnp.concatenate([coords[d] for d in range(dim + 1)], axis=0)
 
     cov, eye = pivot_covariance(dim, coords)
     state[:, 0:ranks] = cov
     state[:, ranks : 2 * ranks] = eye
-    factor_rows(ranks, state)
+    side = pivot_side(dim, coords, centre)
+    local_row = (pivot_row - offset).astype(F32)
+    local_col = jnp.broadcast_to(local_row, (SUB, ranks)).T[:, 0:1].astype(jnp.int32)
+
+    def cross_chunk(c):
+        if c >= width // chunk:
+            return
+        at = slice(c * chunk, (c + 1) * chunk)
+        cross = jnp.exp(jnp.dot(side, sides[:, at], preferred_element_type=F32))
+        ids = lax.broadcasted_iota(jnp.int32, (ranks, chunk), 1) + c * chunk
+        cross = cross + jnp.where(ids == local_col, noise[:, at], 0.0)
+        high = cross.astype(BF16)
+        rest = cross - high.astype(F32)
+        mid = rest.astype(BF16)
+        pieces[0:ranks, at] = high
+        pieces[ranks : 2 * ranks, at] = mid
+        pieces[2 * ranks : 3 * ranks, at] = (rest - mid.astype(F32)).astype(BF16)
+
+    rounds = ranks // (2 * SUB)
+    each = -(-(width // chunk) // rounds)
+
+    def between(r):
+        for c in range(r * each, (r + 1) * each):
+            cross_chunk(c)
+
+    factor_rows(ranks, state, between)
     row = lax.broadcasted_iota(jnp.int32, (ranks, ranks), 0)
     col = lax.broadcasted_iota(jnp.int32, (ranks, ranks), 1)
     solve = jnp.where(row >= col, state[:, ranks : 2 * ranks], 0.0)
-
-    centre = jnp.sum(coords[0:dim, :], axis=1, keepdims=True) / ranks
-    side = pivot_side(dim, coords, centre)
-    local_row = (pivot_row - offset).astype(F32)
-    local_col = jnp.broadcast_to(local_row, (SUB, ranks)).T[:, 0:1].astype(jnp.int32)
+    sh, sm, sl = (x.astype(BF16) for x in split3(solve))
+    lefts = [jnp.concatenate(pair, axis=1) for pair in [(sh, sh), (sm, sm), (sl, sh)]]
+
+    totals = [jnp.zeros((SUB, LANES), F32) for _ in range(blocks)]
     for c in range(width // chunk):
         at = slice(c * chunk, (c + 1) * chunk)
-        x = packed[0:dim, at] - centre
-        cross = jnp.exp(jnp.dot(side, point_side(dim, x), preferred_element_type=F32))
-        noise_row = packed[dim : dim + 1, at]
-        ids = lax.broadcasted_iota(jnp.int32, (ranks, chunk), 1) + c * chunk
-        cross = cross + jnp.where(ids == local_col, noise_row, 0.0)
-        rows = jnp.dot(
-            solve, cross, precision=lax.Precision.HIGHEST, preferred_element_type=F32
+        one = pieces[0 : 2 * ranks, at]
+        two = jnp.concatenate(
+            [pieces[0:ranks, at], pieces[2 * ranks : 3 * ranks, at]], axis=0
+        )
+        rows = (
+            jnp.dot(lefts[0], one, preferred_element_type=F32)
+            + jnp.dot(lefts[1], one, preferred_element_type=F32)
+            + jnp.dot(lefts[2], two, preferred_element_type=F32)
         )
         factor[:, at] = rows
-        left = 1.0 + noise_row
+        square = rows * rows
+        explained = jnp.zeros((SUB, chunk), F32)
         for b in range(blocks):
-            part = rows[b * per_block : (b + 1) * per_block]
-            left = left - jnp.sum(part * part, axis=0, keepdims=True)
-            after[b : b + 1, at] = left
+            part = jnp.zeros((SUB, chunk), F32)
+            for i in range(b * per_block, (b + 1) * per_block, SUB):
+                part = part + square[i : i + SUB]
+            explained = explained + part
+            for j in range(0, chunk, LANES):
+                totals[b] = totals[b] + part[:, j : j + LANES]
+        left = 1.0 + noise[:, at] - jnp.sum(explained, axis=0, keepdims=True)
         residual[at] = left[0]
 
-    total = jnp.zeros((blocks, LANES), F32)
-    for c in range(width // LANES):
-        total = total + after[:, c * LANES : (c + 1) * LANES]
+    total = jnp.concatenate([jnp.sum(x, axis=0, keepdims=True) for x in totals], axis=0)
     total = jnp.sum(total, axis=1, keepdims=True)
     row = lax.broadcasted_iota(jnp.int32, (blocks, LANES), 0)
     col = lax.broadcasted_iota(jnp.int32, (blocks, LANES), 1)
-    near_sums[0] = jnp.sum(jnp.where(row == col, total, 0.0), axis=0, keepdims=True)
-    third = (near, near_sums, send_sem.at[2], recv_sem.at[2])
-    fourth = (far, far_sums, send_sem.at[3], recv_sem.at[3])
-    exchange(*third)
-    all_of(*third).wait_recv()
-    far_sums[0] = total_of(near_sums)
-    exchange(*fourth)
-    all_of(*fourth).wait_recv()
-    total = total_of(far_sums)
-    for step in (first, second, third, fourth):
-        all_of(*step).wait_send()
-    averages[...] = total[0, 0:blocks] / (width * n)
+    done = jnp.sum(jnp.where(row <= col, total, 0.0), axis=0, keepdims=True)
+    sum_slots[0] = base - done
+
+    def send_sum(k, carry):
+        send(sum_slots, k, lax.rem(me + k, n), send_sem.at[2], recv_sem.at[2])
+        return carry
+
+    lax.fori_loop(1, n, send_sum, 0)
+    last = all_of(sum_slots, near[0], send_sem.at[2], recv_sem.at[2])
+    all_of(near_slots, near[0], send_sem.at[0], recv_sem.at[0]).wait_send()
+    all_of(far_slots, far[0], send_sem.at[1], recv_sem.at[1]).wait_send()
+    last.wait_send()
+    last.wait_recv()
+    averages[...] = total_of(sum_slots)[0, 0:blocks] / (width * n)
 
 
 def store_kernel(factor, residual, averages, to_factor, to_residual, to_averages, sem):
@@ -303,6 +370,7 @@
     while group * group < n:
         group *= 2
     vmem = pl.BlockSpec(memory_space=pltpu.VMEM)
+    anywhere = pl.BlockSpec(memory_space=pl.ANY)
     factor, residual, averages = pl.pallas_call(
         functools.partial(body_kernel, n, group, blocks, chunk),
         name="whole",
@@ -311,24 +379,27 @@
             pltpu.VMEM((width,), F32),
             pltpu.VMEM((blocks,), F32),
         ),
-        in_specs=[
-            vmem, pl.BlockSpec(memory_space=pltpu.SMEM), vmem, vmem, vmem,
-        ],
+        in_specs=[anywhere] * 5,
         out_specs=(vmem, vmem, vmem),
         scratch_shapes=[
-            pltpu.VMEM((2 * dim, width), F32),
+            pltpu.VMEM((dim, width), F32),
+            pltpu.SMEM((dim,), F32),
+            pltpu.VMEM((1, width), F32),
+            pltpu.VMEM((width // LANES, LANES), F32),
+            pltpu.VMEM(pivots.shape, jnp.int32),
             pltpu.VMEM((group, dim + 1, 1, ranks), F32),
             pltpu.VMEM((n // group, dim + 1, 1, ranks), F32),
+            pltpu.VMEM((n, 1, LANES), F32),
             pltpu.VMEM((ranks, 2 * ranks), F32),
-            pltpu.VMEM((blocks, width), F32),
-            pltpu.VMEM((group, 1, LANES), F32),
-            pltpu.VMEM((n // group, 1, LANES), F32),
-            pltpu.SemaphoreType.DMA((4,)),
-            pltpu.SemaphoreType.DMA((4,)),
+            pltpu.VMEM((8 * dim, width), BF16),
+            pltpu.VMEM((3 * ranks, width), BF16),
+            pltpu.SemaphoreType.DMA((5,)),
+            pltpu.SemaphoreType.DMA((3,)),
+            pltpu.SemaphoreType.DMA((3,)),
+            pltpu.SemaphoreType.REGULAR,
         ],
         compiler_params=pltpu.CompilerParams(collective_id=0, has_side_effects=True),
     )(points, scales, noise_var.reshape(1, -1), noise_var.reshape(-1, LANES), pivots)
-    anywhere = pl.BlockSpec(memory_space=pl.ANY)
     return pl.pallas_call(
         store_kernel,
         name="store",

time: 29.8 us -> 23.8 us (0.80)
  Pallas kernels: 29 us -> 23 us
    pallas_call x1, Pallas kernels: 27.7 us -> 21.7 us  [body(): pl.pallas_call(functools.partial(body_kernel, n, group, blocks, chunk), n...]
where the time goes in v2:
time: 23.8 us; the launch traced here: 23.7 us
  Pallas kernels  23 us (97%)
  between operations  0.64 us (3%)
    pallas_call x1, Pallas kernels, body(): pl.pallas_call(functools.partial(body_kernel, n, group, blocks, chunk), n...  21.7 us
    pallas_call x1, Pallas kernels, body(): pl.pallas_call(store_kernel, name='store', out_shape=(jax.ShapeDtypeStruc...  1.35 us

profile of v2, /device:TPU:0, one launch (start us, length us, event | category | flops | bytes accessed | tf_op | source)
XLA Modules:
  0.0 23.7 jit_solution(12516496342944873350)
XLA Ops:
  0.6 21.7 %whole.1 = (f32[128,4096]{1,0:T(8,128)S(1)}, f32[4096]{0:T(1024)S(1)}, f32[8]{0:T(128)S(1)}) custom-call(f32[8,4096]{1,0:T(8,128)} %from_points.1, f32[8]{0:T(128)} %from_scales.1, f32[1,4096]{1,0:T(1,128)} %bitcast.2, f32[32,128]{1,0:T(8,128)} %bitcast.3, s32[8,16]{1,0:T(8,128)} %from_pivots.1), custom_call_target="tpu_custom_call" | custom-call | tf_op jit(solution)/shard_map/whole/pallas_call | solution.py:374
  22.3 1.4 %store.1 = (f32[128,4096]{1,0:T(8,128)}, f32[4096]{0:T(1024)}, f32[8]{0:T(128)}) custom-call(f32[128,4096]{1,0:T(8,128)S(1)} %get-tuple-element.6.factor, f32[4096]{0:T(1024)S(1)} %get-tuple-element.7.residual, f32[8]{0:T(128)S(1)} %get-tuple-element.8.averages), custom_call_target="tpu_custom_call" | custom-call | tf_op jit(solution)/shard_map/store/pallas_call | solution.py:403

commit v3 on v2

--- a/solution.py
+++ b/solution.py
@@ -1,4 +1,5 @@
 import functools
+import math
 
 import jax
 import jax.numpy as jnp
@@ -11,6 +12,7 @@
 SUB = 8
 F32 = jnp.float32
 BF16 = jnp.bfloat16
+LOG2E = math.log2(math.e)
 
 
 def split3(x):
@@ -58,86 +60,99 @@
         total = total + differ * differ
     row = lax.broadcasted_iota(jnp.int32, (ranks, ranks), 0)
     col = lax.broadcasted_iota(jnp.int32, (ranks, ranks), 1)
-    cov = jnp.exp(-0.5 * total) + jnp.where(row == col, coords[dim : dim + 1, :], 0.0)
-    return cov, (row == col).astype(F32)
-
-
-def eliminate(left, right, first_lane):
-    shape = left[0].shape
-    a = [
-        [
-            jnp.broadcast_to(left[i][:, first_lane + j : first_lane + j + 1], shape)
-            for j in range(i + 1)
+    return jnp.exp(-0.5 * total) + jnp.where(row == col, coords[dim : dim + 1, :], 0.0)
+
+
+def over_rows(x, i):
+    return jnp.broadcast_to(x[i % SUB : i % SUB + 1], x.shape)
+
+
+def over_lanes(x, j):
+    return jnp.broadcast_to(x[:, j : j + 1], x.shape)
+
+
+def eliminate(rows, cols, low_rows, low_cols):
+    size = SUB * len(rows)
+    diag = over_rows(cols[0][0], 0)
+    done = []
+    for k in range(size):
+        own = k // SUB
+        r = lax.rsqrt(diag)
+        if k + 1 < size:
+            after = (k + 1) // SUB
+            step = over_rows(cols[k][after], k + 1) * r
+            diag = over_rows(cols[k + 1][after], k + 1) - step * step
+        unit = over_rows(rows[own], k) * r
+        done.append(unit)
+        col = [cols[k][v] * r if v >= own else None for v in range(len(rows))]
+        low_col = [x * r for x in low_cols[k]]
+        for j in range(k + 1, size):
+            m = over_rows(col[j // SUB], j)
+            for v in range(j // SUB, len(rows)):
+                cols[j][v] = cols[j][v] - col[v] * m
+            for v in range(len(low_rows)):
+                low_cols[j][v] = low_cols[j][v] - low_col[v] * m
+        for v in range((k + 1) // SUB, len(rows)):
+            rows[v] = rows[v] - col[v] * unit
+        for v in range(len(low_rows)):
+            low_rows[v] = low_rows[v] - low_col[v] * unit
+    return [
+        jnp.concatenate([done[i][i % SUB : i % SUB + 1] for i in range(v, v + SUB)], axis=0)
+        for v in range(0, size, SUB)
+    ]
+
+
+def outer_update(done, hi):
+    h, m, l = split3(jnp.concatenate(done, axis=0))
+    one = jnp.concatenate([h, h, h, m, m, l], axis=0).T[hi:].astype(BF16)
+    two = jnp.concatenate([h, m, l, h, m, h], axis=0).astype(BF16)
+    return jnp.dot(one, two, preferred_element_type=F32)
+
+
+def factor_rows(ranks, state, between):
+    size = 2 * SUB
+    row = lax.broadcasted_iota(jnp.int32, (SUB, ranks), 0)
+    col = lax.broadcasted_iota(jnp.int32, (SUB, ranks), 1)
+
+    def columns(rows, at):
+        return [
+            [over_lanes(x, j) if at + v * SUB + SUB > j else None for v, x in enumerate(rows)]
+            for j in range(at, at + size)
         ]
-        for i in range(SUB)
-    ]
-    inverse = []
-    for k in range(SUB):
-        r = lax.rsqrt(a[k][k])
-        inverse.append(r)
-        left[k] = left[k] * r
-        right[k] = right[k] * r
-        for i in range(k + 1, SUB):
-            a[i][k] = a[i][k] * r
-        for i in range(k + 1, SUB):
-            for j in range(k + 1, i + 1):
-                a[i][j] = a[i][j] - a[i][k] * a[j][k]
-            left[i] = left[i] - a[i][k] * left[k]
-            right[i] = right[i] - a[i][k] * right[k]
-    return a, inverse
-
-
-def spread(rows):
-    return [jnp.broadcast_to(rows[i : i + 1], rows.shape) for i in range(SUB)]
-
-
-def gathered(rows):
-    return jnp.concatenate([rows[i][i : i + 1] for i in range(SUB)], axis=0)
-
-
-def factor_rows(ranks, state, between):
-    step = 2 * SUB
-    for lo in range(0, ranks, step):
-        mid, hi = lo + SUB, lo + step
-        left = spread(state[lo:mid, 0:ranks])
-        right = spread(state[lo:mid, ranks : 2 * ranks])
-        low_left = state[mid:hi, 0:ranks]
-        low_right = state[mid:hi, ranks : 2 * ranks]
-        start = [
-            jnp.broadcast_to(low_left[:, lo + k : lo + k + 1], (SUB, ranks))
-            for k in range(SUB)
+
+    def opened(rows, first, at):
+        inside = jnp.logical_and(col >= at, col < at + size)
+        return [
+            jnp.where(inside, jnp.where(row + (first + v * SUB) == col, 1.0, 0.0), x)
+            for v, x in enumerate(rows)
         ]
-        mult, inverse = eliminate(left, right, lo)
-        cols = []
-        for k in range(SUB):
-            col = start[k]
-            for j in range(k):
-                col = col - cols[j] * mult[k][j]
-            cols.append(col * inverse[k])
-        for k in range(SUB):
-            low_left = low_left - cols[k] * left[k]
-            low_right = low_right - cols[k] * right[k]
-        next_left, next_right = spread(low_left), spread(low_right)
-        eliminate(next_left, next_right, mid)
-        new_left = jnp.concatenate([gathered(left), gathered(next_left)], axis=0)
-        new_right = jnp.concatenate([gathered(right), gathered(next_right)], axis=0)
-        state[lo:hi, ranks : 2 * ranks] = new_right
+
+    for lo in range(0, ranks, 2 * size):
+        mid, hi = lo + size, lo + 2 * size
+        rows = [state[i : i + SUB, :] for i in range(lo, mid, SUB)]
+        low_rows = [state[i : i + SUB, :] for i in range(mid, hi, SUB)]
+        cols = columns(rows, lo)
+        low_cols = [[over_lanes(x, j) for x in low_rows] for j in range(lo, mid)]
+        rows, low_rows = opened(rows, lo, lo), opened(low_rows, mid, lo)
+        first = eliminate(rows, cols, low_rows, low_cols)
+        first = [jnp.where(jnp.logical_and(col >= mid, col < hi), 0.0, x) for x in first]
+        cols = columns(low_rows, mid)
+        low_rows = opened(low_rows, mid, mid)
+        second = eliminate(low_rows, cols, [], [[] for _ in range(size)])
+        for v, x in enumerate(first + second):
+            state[lo + v * SUB : lo + v * SUB + SUB, :] = x
         if hi < ranks:
-            new = jnp.concatenate([new_left, new_right], axis=1)
-            h, m, l = split3(new)
-            lh, lm, ll = (x[:, 0:ranks] for x in (h, m, l))
-            one = jnp.concatenate([lh, lh, lh, lm, lm, ll], axis=0).T[hi:ranks].astype(BF16)
-            two = jnp.concatenate([h, m, l, h, m, h], axis=0).astype(BF16)
-            state[hi:ranks, :] = state[hi:ranks, :] - jnp.dot(
-                one, two, preferred_element_type=F32
-            )
-        between(lo // step)
+            update = outer_update(first, hi) + outer_update(second, hi)
+            wide = lax.broadcasted_iota(jnp.int32, update.shape, 1)
+            kept = jnp.where(jnp.logical_and(wide >= lo, wide < hi), 0.0, state[hi:, :])
+            state[hi:, :] = kept - update
+        between(lo // (2 * size))
 
 
 def pivot_side(dim, coords, centre):
     y = coords[0:dim, :] - centre
-    yh, ym, yl = split3(y)
-    nh, nm, nl = split3(-0.5 * jnp.sum(y * y, axis=0, keepdims=True))
+    yh, ym, yl = split3(LOG2E * y)
+    nh, nm, nl = split3((-0.5 * LOG2E) * jnp.sum(y * y, axis=0, keepdims=True))
     ones = jnp.ones_like(nh)
     tail = [ones, ones, ones, nh, nm, nl, jnp.zeros((2 * dim - 6, y.shape[1]), F32)]
     return jnp.concatenate([yh, yh, ym, ym, yh, yl] + tail, axis=0).T.astype(BF16)
@@ -145,7 +160,7 @@
 
 def point_side(dim, x):
     xh, xm, xl = split3(x)
-    nh, nm, nl = split3(-0.5 * jnp.sum(x * x, axis=0, keepdims=True))
+    nh, nm, nl = split3((-0.5 * LOG2E) * jnp.sum(x * x, axis=0, keepdims=True))
     ones = jnp.ones_like(nh)
     tail = [nh, nm, nl, ones, ones, ones, jnp.zeros((2 * dim - 6, x.shape[1]), F32)]
     return jnp.concatenate([xh, xm, xh, xm, xl, xh] + tail, axis=0).astype(BF16)
@@ -268,9 +283,7 @@
     coords = total_of(far_slots)
     coords = jnp.concatenate([coords[d] for d in range(dim + 1)], axis=0)
 
-    cov, eye = pivot_covariance(dim, coords)
-    state[:, 0:ranks] = cov
-    state[:, ranks : 2 * ranks] = eye
+    state[...] = pivot_covariance(dim, coords)
     side = pivot_side(dim, coords, centre)
     local_row = (pivot_row - offset).astype(F32)
     local_col = jnp.broadcast_to(local_row, (SUB, ranks)).T[:, 0:1].astype(jnp.int32)
@@ -279,17 +292,14 @@
         if c >= width // chunk:
             return
         at = slice(c * chunk, (c + 1) * chunk)
-        cross = jnp.exp(jnp.dot(side, sides[:, at], preferred_element_type=F32))
+        cross = jnp.exp2(jnp.dot(side, sides[:, at], preferred_element_type=F32))
         ids = lax.broadcasted_iota(jnp.int32, (ranks, chunk), 1) + c * chunk
-        cross = cross + jnp.where(ids == local_col, noise[:, at], 0.0)
+        cross = jnp.where(ids == local_col, 1.0 + noise[:, at], cross)
         high = cross.astype(BF16)
-        rest = cross - high.astype(F32)
-        mid = rest.astype(BF16)
         pieces[0:ranks, at] = high
-        pieces[ranks : 2 * ranks, at] = mid
-        pieces[2 * ranks : 3 * ranks, at] = (rest - mid.astype(F32)).astype(BF16)
-
-    rounds = ranks // (2 * SUB)
+        pieces[ranks : 2 * ranks, at] = (cross - high.astype(F32)).astype(BF16)
+
+    rounds = ranks // (4 * SUB)
     each = -(-(width // chunk) // rounds)
 
     def between(r):
@@ -299,21 +309,19 @@
     factor_rows(ranks, state, between)
     row = lax.broadcasted_iota(jnp.int32, (ranks, ranks), 0)
     col = lax.broadcasted_iota(jnp.int32, (ranks, ranks), 1)
-    solve = jnp.where(row >= col, state[:, ranks : 2 * ranks], 0.0)
-    sh, sm, sl = (x.astype(BF16) for x in split3(solve))
-    lefts = [jnp.concatenate(pair, axis=1) for pair in [(sh, sh), (sm, sm), (sl, sh)]]
+    solve = jnp.where(row >= col, state[...], 0.0)
+    high = solve.astype(BF16)
+    lefts = [
+        jnp.concatenate([x, x], axis=1)
+        for x in (high, (solve - high.astype(F32)).astype(BF16))
+    ]
 
     totals = [jnp.zeros((SUB, LANES), F32) for _ in range(blocks)]
     for c in range(width // chunk):
         at = slice(c * chunk, (c + 1) * chunk)
-        one = pieces[0 : 2 * ranks, at]
-        two = jnp.concatenate(
-            [pieces[0:ranks, at], pieces[2 * ranks : 3 * ranks, at]], axis=0
-        )
-        rows = (
-            jnp.dot(lefts[0], one, preferred_element_type=F32)
-            + jnp.dot(lefts[1], one, preferred_element_type=F32)
-            + jnp.dot(lefts[2], two, preferred_element_type=F32)
+        one = pieces[:, at]
+        rows = jnp.dot(lefts[0], one, preferred_element_type=F32) + jnp.dot(
+            lefts[1], one, preferred_element_type=F32
         )
         factor[:, at] = rows
         square = rows * rows
@@ -390,9 +398,9 @@
             pltpu.VMEM((group, dim + 1, 1, ranks), F32),
             pltpu.VMEM((n // group, dim + 1, 1, ranks), F32),
             pltpu.VMEM((n, 1, LANES), F32),
-            pltpu.VMEM((ranks, 2 * ranks), F32),
+            pltpu.VMEM((ranks, ranks), F32),
             pltpu.VMEM((8 * dim, width), BF16),
-            pltpu.VMEM((3 * ranks, width), BF16),
+            pltpu.VMEM((2 * ranks, width), BF16),
             pltpu.SemaphoreType.DMA((5,)),
             pltpu.SemaphoreType.DMA((3,)),
             pltpu.SemaphoreType.DMA((3,)),

time: 23.8 us -> 22 us (0.924)
  Pallas kernels: 23 us -> 21.2 us
    pallas_call x1, Pallas kernels: 21.7 us -> 19.8 us  [body(): pl.pallas_call(functools.partial(body_kernel, n, group, blocks, chunk), n...]
where the time goes in v3:
time: 22 us; the launch traced here: 21.8 us
  Pallas kernels  21.2 us (96%)
  between operations  0.64 us (3%)
    pallas_call x1, Pallas kernels, body(): pl.pallas_call(functools.partial(body_kernel, n, group, blocks, chunk), n...  19.8 us
    pallas_call x1, Pallas kernels, body(): pl.pallas_call(store_kernel, name='store', out_shape=(jax.ShapeDtypeStruc...  1.35 us

profile of v3, /device:TPU:0, one launch (start us, length us, event | category | flops | bytes accessed | tf_op | source)
XLA Modules:
  0.0 21.8 jit_solution(2295670690087439400)
XLA Ops:
  0.6 19.8 %whole.1 = (f32[128,4096]{1,0:T(8,128)S(1)}, f32[4096]{0:T(1024)S(1)}, f32[8]{0:T(128)S(1)}) custom-call(f32[8,4096]{1,0:T(8,128)} %from_points.1, f32[8]{0:T(128)} %from_scales.1, f32[1,4096]{1,0:T(1,128)} %bitcast.2, f32[32,128]{1,0:T(8,128)} %bitcast.3, s32[8,16]{1,0:T(8,128)} %from_pivots.1), custom_call_target="tpu_custom_call" | custom-call | tf_op jit(solution)/shard_map/whole/pallas_call | solution.py:382
  20.5 1.4 %store.1 = (f32[128,4096]{1,0:T(8,128)}, f32[4096]{0:T(1024)}, f32[8]{0:T(128)}) custom-call(f32[128,4096]{1,0:T(8,128)S(1)} %get-tuple-element.6.factor, f32[4096]{0:T(1024)S(1)} %get-tuple-element.7.residual, f32[8]{0:T(128)S(1)} %get-tuple-element.8.averages), custom_call_target="tpu_custom_call" | custom-call | tf_op jit(solution)/shard_map/store/pallas_call | solution.py:411

commit v4 on v3

--- a/solution.py
+++ b/solution.py
@@ -71,10 +71,17 @@
     return jnp.broadcast_to(x[:, j : j + 1], x.shape)
 
 
-def eliminate(rows, cols, low_rows, low_cols):
+def gathered(rows):
+    return [
+        jnp.concatenate([rows[i][i % SUB : i % SUB + 1] for i in range(v, v + SUB)], axis=0)
+        for v in range(0, len(rows), SUB)
+    ]
+
+
+def factor_block(rows, cols):
     size = SUB * len(rows)
     diag = over_rows(cols[0][0], 0)
-    done = []
+    scales, factors, units = [], [], []
     for k in range(size):
         own = k // SUB
         r = lax.rsqrt(diag)
@@ -83,70 +90,93 @@
             step = over_rows(cols[k][after], k + 1) * r
             diag = over_rows(cols[k + 1][after], k + 1) - step * step
         unit = over_rows(rows[own], k) * r
-        done.append(unit)
-        col = [cols[k][v] * r if v >= own else None for v in range(len(rows))]
-        low_col = [x * r for x in low_cols[k]]
+        col = [x * r if v >= own else None for v, x in enumerate(cols[k])]
+        factor = {j: over_rows(col[j // SUB], j) for j in range(k + 1, size)}
         for j in range(k + 1, size):
-            m = over_rows(col[j // SUB], j)
             for v in range(j // SUB, len(rows)):
-                cols[j][v] = cols[j][v] - col[v] * m
-            for v in range(len(low_rows)):
-                low_cols[j][v] = low_cols[j][v] - low_col[v] * m
+                cols[j][v] = cols[j][v] - col[v] * factor[j]
         for v in range((k + 1) // SUB, len(rows)):
             rows[v] = rows[v] - col[v] * unit
-        for v in range(len(low_rows)):
-            low_rows[v] = low_rows[v] - low_col[v] * unit
-    return [
-        jnp.concatenate([done[i][i % SUB : i % SUB + 1] for i in range(v, v + SUB)], axis=0)
-        for v in range(0, size, SUB)
-    ]
-
-
-def outer_update(done, hi):
-    h, m, l = split3(jnp.concatenate(done, axis=0))
-    one = jnp.concatenate([h, h, h, m, m, l], axis=0).T[hi:].astype(BF16)
-    two = jnp.concatenate([h, m, l, h, m, h], axis=0).astype(BF16)
-    return jnp.dot(one, two, preferred_element_type=F32)
-
-
-def factor_rows(ranks, state, between):
-    size = 2 * SUB
+        scales.append(r)
+        factors.append(factor)
+        units.append(unit)
+    done = gathered(units)
+    for k in reversed(range(size)):
+        units[k] = units[k] * scales[k]
+        for i in range(k):
+            units[i] = units[i] - factors[i][k] * units[k]
+    return units, done
+
+
+def wide_product(left, right, lo):
+    ranks = left.shape[1]
+    size = right.shape[0]
+    h, m, l = split3(left)
+    rh, rm, rl = (
+        jnp.concatenate(
+            [x for x in (jnp.zeros((lo, ranks), F32), y, jnp.zeros((ranks - lo - size, ranks), F32)) if x.shape[0]],
+            axis=0,
+        )
+        for y in split3(right)
+    )
+    one = jnp.concatenate([rh, rm], axis=0).astype(BF16)
+    two = jnp.concatenate([rh, rl], axis=0).astype(BF16)
+    return (
+        jnp.dot(jnp.concatenate([h, h], axis=1).astype(BF16), one, preferred_element_type=F32)
+        + jnp.dot(jnp.concatenate([m, m], axis=1).astype(BF16), one, preferred_element_type=F32)
+        + jnp.dot(jnp.concatenate([l, h], axis=1).astype(BF16), two, preferred_element_type=F32)
+    )
+
+
+def factor_rows(cov, between):
+    ranks = cov.shape[0]
+    count = 2
+    size = count * SUB
     row = lax.broadcasted_iota(jnp.int32, (SUB, ranks), 0)
     col = lax.broadcasted_iota(jnp.int32, (SUB, ranks), 1)
-
-    def columns(rows, at):
-        return [
-            [over_lanes(x, j) if at + v * SUB + SUB > j else None for v, x in enumerate(rows)]
-            for j in range(at, at + size)
+    rows = [cov[i : i + SUB] for i in range(0, ranks, SUB)]
+    done = []
+    nothing = 0.0 * rows[0]
+    late = None
+    for lo in range(0, ranks, size):
+        if late is not None:
+            rows[count:] = late()
+        inside = jnp.logical_and(col >= lo, col < lo + size)
+        block, near, far = rows[0:count], rows[count : 2 * count], rows[2 * count :]
+        lanes = range(lo, lo + size)
+        cols = [
+            [over_lanes(x, j) if lo + v * SUB + SUB > j else None for v, x in enumerate(block)]
+            for j in lanes
         ]
-
-    def opened(rows, first, at):
-        inside = jnp.logical_and(col >= at, col < at + size)
-        return [
-            jnp.where(inside, jnp.where(row + (first + v * SUB) == col, 1.0, 0.0), x)
-            for v, x in enumerate(rows)
+        cols[0][0] = cols[0][0] + nothing
+        cols[1][0] = cols[1][0] + nothing
+        near_cols = [[over_lanes(x, j) for x in near] for j in lanes]
+        block = [
+            jnp.where(inside, jnp.where(row + (lo + v * SUB) == col, 1.0, 0.0), x)
+            for v, x in enumerate(block)
         ]
-
-    for lo in range(0, ranks, 2 * size):
-        mid, hi = lo + size, lo + 2 * size
-        rows = [state[i : i + SUB, :] for i in range(lo, mid, SUB)]
-        low_rows = [state[i : i + SUB, :] for i in range(mid, hi, SUB)]
-        cols = columns(rows, lo)
-        low_cols = [[over_lanes(x, j) for x in low_rows] for j in range(lo, mid)]
-        rows, low_rows = opened(rows, lo, lo), opened(low_rows, mid, lo)
-        first = eliminate(rows, cols, low_rows, low_cols)
-        first = [jnp.where(jnp.logical_and(col >= mid, col < hi), 0.0, x) for x in first]
-        cols = columns(low_rows, mid)
-        low_rows = opened(low_rows, mid, mid)
-        second = eliminate(low_rows, cols, [], [[] for _ in range(size)])
-        for v, x in enumerate(first + second):
-            state[lo + v * SUB : lo + v * SUB + SUB, :] = x
-        if hi < ranks:
-            update = outer_update(first, hi) + outer_update(second, hi)
-            wide = lax.broadcasted_iota(jnp.int32, update.shape, 1)
-            kept = jnp.where(jnp.logical_and(wide >= lo, wide < hi), 0.0, state[hi:, :])
-            state[hi:, :] = kept - update
-        between(lo // (2 * size))
+        units, new = factor_block(block, cols)
+        done += new
+        rows = []
+        for v, x in enumerate(near):
+            terms = [near_cols[j][v] * units[j] for j in range(size)]
+            while len(terms) > 1:
+                terms = [p + q for p, q in zip(terms[::2], terms[1::2])]
+            rows.append(jnp.where(inside, 0.0, x) - terms[0])
+
+        def late(far=far, units=gathered(units), inside=inside, lo=lo):
+            if not far:
+                return []
+            left = jnp.concatenate([jnp.where(inside, x, 0.0) for x in far], axis=0)
+            out = wide_product(left, jnp.concatenate(units, axis=0), lo)
+            return [
+                jnp.where(inside, 0.0, x) - out[i * SUB : (i + 1) * SUB]
+                for i, x in enumerate(far)
+            ]
+
+        rows += [None] * len(far)
+        between(lo // size, done)
+    return done
 
 
 def pivot_side(dim, coords, centre):
@@ -209,8 +239,8 @@
     from_points, from_scales, from_noise, from_tiles, from_pivots,
     factor, residual, averages,
     points, scales, noise, noise_tiles, pivots,
-    near_slots, far_slots, sum_slots, state, sides, pieces,
-    load_sem, send_sem, recv_sem, ready_sem,
+    near_slots, far_slots, sum_slots, sides, pieces, explained,
+    load_sem, send_sem, recv_sem, ready_sem, near_sent,
 ):
     dim, width = points.shape
     ranks = factor.shape[0]
@@ -254,7 +284,7 @@
     near_slots[0, dim] = own_noise
     pl.semaphore_wait(barrier, group - 1 + level)
     for k, device in enumerate(near):
-        send(near_slots, k + 1, device, send_sem.at[0], recv_sem.at[0])
+        send(near_slots, k + 1, device, near_sent.at[k], recv_sem.at[0])
     for k in range(1, far_count):
 
         @pl.when(level >= k)
@@ -283,7 +313,7 @@
     coords = total_of(far_slots)
     coords = jnp.concatenate([coords[d] for d in range(dim + 1)], axis=0)
 
-    state[...] = pivot_covariance(dim, coords)
+    cov = pivot_covariance(dim, coords)
     side = pivot_side(dim, coords, centre)
     local_row = (pivot_row - offset).astype(F32)
     local_col = jnp.broadcast_to(local_row, (SUB, ranks)).T[:, 0:1].astype(jnp.int32)
@@ -299,41 +329,78 @@
         pieces[0:ranks, at] = high
         pieces[ranks : 2 * ranks, at] = (cross - high.astype(F32)).astype(BF16)
 
-    rounds = ranks // (4 * SUB)
-    each = -(-(width // chunk) // rounds)
-
-    def between(r):
-        for c in range(r * each, (r + 1) * each):
-            cross_chunk(c)
-
-    factor_rows(ranks, state, between)
-    row = lax.broadcasted_iota(jnp.int32, (ranks, ranks), 0)
-    col = lax.broadcasted_iota(jnp.int32, (ranks, ranks), 1)
-    solve = jnp.where(row >= col, state[...], 0.0)
-    high = solve.astype(BF16)
-    lefts = [
-        jnp.concatenate([x, x], axis=1)
-        for x in (high, (solve - high.astype(F32)).astype(BF16))
-    ]
-
+    size = 2 * SUB
+    rounds = ranks // size
+    chunks = range(width // chunk)
     totals = [jnp.zeros((SUB, LANES), F32) for _ in range(blocks)]
-    for c in range(width // chunk):
+    col = lax.broadcasted_iota(jnp.int32, (SUB, ranks), 1)
+    row = lax.broadcasted_iota(jnp.int32, (SUB, ranks), 0)
+
+    def lefts_of(done, top, bottom):
+        part = [
+            jnp.where(row + i * SUB >= col, done[i], 0.0)
+            for i in range(top // SUB, bottom // SUB)
+        ]
+        high, mid, low = split3(jnp.concatenate(part, axis=0))
+        tall = jnp.concatenate([low, mid, high], axis=0)
+        return jnp.concatenate([tall, tall], axis=1).astype(BF16)
+
+    def product(c, lefts, top, bottom):
         at = slice(c * chunk, (c + 1) * chunk)
         one = pieces[:, at]
-        rows = jnp.dot(lefts[0], one, preferred_element_type=F32) + jnp.dot(
-            lefts[1], one, preferred_element_type=F32
-        )
-        factor[:, at] = rows
+        wide = jnp.dot(lefts, one, preferred_element_type=F32)
+        rows = jnp.zeros((bottom - top, chunk), F32)
+        for i in range(0, wide.shape[0], bottom - top):
+            rows = rows + wide[i : i + bottom - top]
+        factor[top:bottom, at] = rows
         square = rows * rows
-        explained = jnp.zeros((SUB, chunk), F32)
-        for b in range(blocks):
+        added = jnp.zeros((SUB, chunk), F32)
+        for b in range(top // per_block, bottom // per_block):
             part = jnp.zeros((SUB, chunk), F32)
-            for i in range(b * per_block, (b + 1) * per_block, SUB):
+            for i in range(b * per_block - top, (b + 1) * per_block - top, SUB):
                 part = part + square[i : i + SUB]
-            explained = explained + part
+            added = added + part
             for j in range(0, chunk, LANES):
                 totals[b] = totals[b] + part[:, j : j + LANES]
-        left = 1.0 + noise[:, at] - jnp.sum(explained, axis=0, keepdims=True)
+        return added
+
+    def sent(k):
+        return pltpu.make_async_remote_copy(
+            src_ref=near_slots.at[0],
+            dst_ref=near_slots.at[k + 1],
+            send_sem=near_sent.at[k],
+            recv_sem=recv_sem.at[0],
+            device_id=(near[k],),
+            device_id_type=pl.DeviceIdType.MESH,
+        )
+
+    early, middle = size * (rounds // 2), size * (rounds - 2)
+
+    def share(r, first, last):
+        each = -(-len(chunks) // (last - first))
+        return chunks[(r - first) * each : (r - first + 1) * each] if first <= r < last else []
+
+    def between(r, done):
+        for c in share(r, 1, rounds // 2 + 1):
+            cross_chunk(c)
+        if rounds // 2 < r < rounds - 1:
+            lefts = lefts_of(done, 0, early)
+            for c in share(r, rounds // 2 + 1, rounds - 1):
+                explained[:, c * chunk : (c + 1) * chunk] = product(c, lefts, 0, early)
+        if r == rounds - 1:
+            lefts = lefts_of(done, early, middle)
+            for c in chunks:
+                at = slice(c * chunk, (c + 1) * chunk)
+                explained[:, at] = explained[:, at] + product(c, lefts, early, middle)
+        if r < min(rounds - 1, len(near)):
+            sent(r).wait_send()
+
+    done = factor_rows(cov, between)
+    lefts = lefts_of(done, middle, ranks)
+    for c in chunks:
+        at = slice(c * chunk, (c + 1) * chunk)
+        added = explained[:, at] + product(c, lefts, middle, ranks)
+        left = 1.0 + noise[:, at] - jnp.sum(added, axis=0, keepdims=True)
         residual[at] = left[0]
 
     total = jnp.concatenate([jnp.sum(x, axis=0, keepdims=True) for x in totals], axis=0)
@@ -349,7 +416,8 @@
 
     lax.fori_loop(1, n, send_sum, 0)
     last = all_of(sum_slots, near[0], send_sem.at[2], recv_sem.at[2])
-    all_of(near_slots, near[0], send_sem.at[0], recv_sem.at[0]).wait_send()
+    for k in range(min(rounds - 1, len(near)), len(near)):
+        sent(k).wait_send()
     all_of(far_slots, far[0], send_sem.at[1], recv_sem.at[1]).wait_send()
     last.wait_send()
     last.wait_recv()
@@ -398,13 +466,14 @@
             pltpu.VMEM((group, dim + 1, 1, ranks), F32),
             pltpu.VMEM((n // group, dim + 1, 1, ranks), F32),
             pltpu.VMEM((n, 1, LANES), F32),
-            pltpu.VMEM((ranks, ranks), F32),
             pltpu.VMEM((8 * dim, width), BF16),
             pltpu.VMEM((2 * ranks, width), BF16),
+            pltpu.VMEM((SUB, width), F32),
             pltpu.SemaphoreType.DMA((5,)),
             pltpu.SemaphoreType.DMA((3,)),
             pltpu.SemaphoreType.DMA((3,)),
             pltpu.SemaphoreType.REGULAR,
+            pltpu.SemaphoreType.DMA((group - 1,)),
         ],
         compiler_params=pltpu.CompilerParams(collective_id=0, has_side_effects=True),
     )(points, scales, noise_var.reshape(1, -1), noise_var.reshape(-1, LANES), pivots)

time: 22 us -> 21.8 us (level)
  no operation moved by 1% of the time
where the time goes in v4:
time: 21.8 us; the launch traced here: 21.7 us
  Pallas kernels  21 us (96%)
  between operations  0.64 us (3%)
    pallas_call x1, Pallas kernels, body(): pl.pallas_call(functools.partial(body_kernel, n, group, blocks, chunk), n...  19.7 us
    pallas_call x1, Pallas kernels, body(): pl.pallas_call(store_kernel, name='store', out_shape=(jax.ShapeDtypeStruc...  1.35 us

profile of v4, /device:TPU:0, one launch (start us, length us, event | category | flops | bytes accessed | tf_op | source)
XLA Modules:
  0.0 21.7 jit_solution(1609336132452821054)
XLA Ops:
  0.6 19.7 %whole.1 = (f32[128,4096]{1,0:T(8,128)S(1)}, f32[4096]{0:T(1024)S(1)}, f32[8]{0:T(128)S(1)}) custom-call(f32[8,4096]{1,0:T(8,128)} %from_points.1, f32[8]{0:T(128)} %from_scales.1, f32[1,4096]{1,0:T(1,128)} %bitcast.2, f32[32,128]{1,0:T(8,128)} %bitcast.3, s32[8,16]{1,0:T(8,128)} %from_pivots.1), custom_call_target="tpu_custom_call" | custom-call | tf_op jit(solution)/shard_map/whole/pallas_call | solution.py:450
  20.3 1.4 %store.1 = (f32[128,4096]{1,0:T(8,128)}, f32[4096]{0:T(1024)}, f32[8]{0:T(128)}) custom-call(f32[128,4096]{1,0:T(8,128)S(1)} %get-tuple-element.6.factor, f32[4096]{0:T(1024)S(1)} %get-tuple-element.7.residual, f32[8]{0:T(128)S(1)} %get-tuple-element.8.averages), custom_call_target="tpu_custom_call" | custom-call | tf_op jit(solution)/shard_map/store/pallas_call | solution.py:480
